TPU v7x, 256 devices: a whole 4x4x8 slice. The times are simulated.
256 devices in a mesh: dom: 128 (over x, y, z), sub: 2 (over core).
Axes of the slice: x: 4, y: 4, z: 8, core: 2. Of those that a mesh axis runs over, the one named last changes fastest.
Arguments:
- old_states: bfloat16 [4096, 320], P(('dom', 'sub')), may hold values from -6 to 6
- send_elem: int32 [256, 9, 8], P(('dom', 'sub')), may hold values from -1 to 15, as said below
- recv_slot: int32 [4096, 4], P(('dom', 'sub')), may hold values from -1 to 71, as said below
- intersection_count: int32 [4096], P(('dom', 'sub')), may hold values from 1 to 4
- intersection_weight: float32 [4096, 4], P(('dom', 'sub')), may hold values from 0.1 to 1
- interior_inverse: bfloat16 [4096, 320, 320], P(('dom', 'sub')), may hold values from -0.3125 to 0.3125
- inner_coupling: bfloat16 [4096, 320, 400], P(('dom', 'sub')), may hold values from -6 to 6
- face_coupling: bfloat16 [4096, 400, 320], P(('dom', 'sub')), may hold values from -0.3125 to 0.3125
- face_mass: float32 [80, 80], replicated, may hold values from -6 to 6
- face_scale: float32 [4096, 5], P(('dom', 'sub')), may hold values from 0.5 to 2
- face_shift: int32 [4096, 5], P(('dom', 'sub')), may hold values from -4 to 4, as said below
- owner_row: int32 [256, 9, 9], P(('dom', 'sub')), may hold values from -1 to 39, as said below
Outputs:
- face_schur: float32 [10240, 6400], P(('dom', 'sub'))
- face_rhs: float32 [10240, 80], P(('dom', 'sub'))
Inputs may be any that keep to these rules, and one draw needn't show every extreme that they name: `send_elem`: -1 marks an empty slot. For every live entry of recv_slot the named slot holds an element of the source; no slot is named twice; some old owner fills all 8 slots toward one new owner. `recv_slot`: entry k of new element n is -1 exactly when k >= intersection_count[n], else the index of a filled slot. `face_shift`: on one device at most 9 items share a shift value, and some value has exactly 9. `owner_row`: -1 exactly where no item arrives; every owned row is named by exactly two arriving items.
All inputs are finite; a program needn't handle non-finite values.
Results may differ from a plain program's by a relative error of at most 0.0046.
Values may be sent and summed in bfloat16 or wider, within the bound.
A program may use at most 192 MiB of HBM per device.

v0:
```python
import jax
import jax.numpy as jnp
from jax import lax
from jax.sharding import PartitionSpec as P

HIGH = lax.Precision.HIGHEST


def passed_along(block, axis, distance):
    devices = range(lax.axis_size(axis))
    route = [((i - distance) % len(devices), i) for i in devices]
    return lax.ppermute(block, axis, route)


def pick_rows(table, lookup):
    chosen = jnp.take(table, jnp.maximum(lookup, 0), axis=0)
    keep = (lookup >= 0).reshape(lookup.shape + (1,) * (chosen.ndim - lookup.ndim))
    return jnp.where(keep, chosen, jnp.zeros_like(chosen))


def slot_items(slot_of, slot_total):
    item_total = slot_of.shape[0]
    hits = slot_of[None, :] == jnp.arange(slot_total, dtype=jnp.int32)[:, None]
    labels = jnp.arange(item_total, dtype=jnp.int32)[None, :] + 1
    return jnp.sum(jnp.where(hits, labels, 0), axis=1) - 1


def same_shift_rank(shifts):
    item_total = shifts.shape[0]
    order = jnp.arange(item_total, dtype=jnp.int32)
    same = shifts[:, None] == shifts[None, :]
    before = order[None, :] < order[:, None]
    return jnp.sum(jnp.where(same & before, 1, 0), axis=1).astype(jnp.int32)


def per_device(
    old_states,
    send_elem,
    recv_slot,
    intersection_count,
    intersection_weight,
    interior_inverse,
    inner_coupling,
    face_coupling,
    face_mass,
    face_scale,
    face_shift,
    owner_row,
):
    local_send = send_elem[0]
    local_rows = owner_row[0]
    offset_count = local_send.shape[0]
    max_shift = (offset_count - 1) // 2
    bucket_slots = local_send.shape[1]
    element_count, interior_size = old_states.shape
    outgoing = pick_rows(old_states, local_send)
    arrivals = []
    for offset in range(offset_count):
        if offset == max_shift:
            arrivals.append(outgoing[offset])
        else:
            arrivals.append(passed_along(outgoing[offset], "dom", offset - max_shift))
    flat_states = jnp.stack(arrivals, axis=0).reshape(offset_count * bucket_slots, interior_size)
    gathered = pick_rows(flat_states, recv_slot).astype(jnp.float32)
    is_live = jnp.arange(recv_slot.shape[1], dtype=jnp.int32)[None, :] < intersection_count[:, None]
    weights = jnp.where(is_live, intersection_weight, 0.0)
    weight_total = jnp.sum(weights, axis=1, keepdims=True)
    projected = (jnp.einsum("ek,ekr->er", weights, gathered, precision=HIGH) / weight_total).astype(
        jnp.bfloat16
    )
    face_count = face_scale.shape[1]
    face_size = face_mass.shape[0]
    mapped = jnp.einsum(
        "eab,ebc->eac", interior_inverse, inner_coupling, preferred_element_type=jnp.float32
    ).astype(jnp.bfloat16)
    interior_load = jnp.einsum(
        "eab,eb->ea", interior_inverse, projected, preferred_element_type=jnp.float32
    ).astype(jnp.bfloat16)
    rows_in = face_coupling.reshape(element_count, face_count, face_size, interior_size)
    columns = mapped.reshape(element_count, interior_size, face_count, face_size)
    correction = jnp.einsum("ejar,erjb->ejab", rows_in, columns, preferred_element_type=jnp.float32)
    condensed = jnp.einsum(
        "ejar,er->eja", rows_in, interior_load, preferred_element_type=jnp.float32
    )
    schur_block = (face_scale[:, :, None, None] * face_mass[None, None] - correction).astype(
        jnp.bfloat16
    )
    right_side = (-condensed).astype(jnp.bfloat16)
    item_count = element_count * face_count
    payload = jnp.concatenate(
        [
            schur_block.reshape(item_count, face_size * face_size),
            right_side.reshape(item_count, face_size),
        ],
        axis=1,
    )
    shifts = face_shift.reshape(item_count)
    slot_rank = same_shift_rank(shifts)
    bucket_size = local_rows.shape[1]
    sources = slot_items((shifts + max_shift) * bucket_size + slot_rank, offset_count * bucket_size)
    packed = pick_rows(payload, sources).reshape(offset_count, bucket_size, payload.shape[1])
    pieces = []
    for offset in range(offset_count):
        if offset == max_shift:
            pieces.append(packed[offset])
        else:
            pieces.append(passed_along(packed[offset], "dom", offset - max_shift))
    received = jnp.stack(pieces, axis=0)
    owned_rows = local_rows.reshape(offset_count * bucket_size)
    owned_count = item_count // 2
    onehot = (owned_rows[None, :] == jnp.arange(owned_count, dtype=jnp.int32)[:, None]).astype(
        jnp.bfloat16
    )
    summed = jnp.dot(
        onehot,
        received.reshape(offset_count * bucket_size, payload.shape[1]),
        preferred_element_type=jnp.float32,
    )
    return (summed[:, : face_size * face_size], summed[:, face_size * face_size :])


def solution(mesh):
    in_specs = (
        P(("dom", "sub"), None),
        P(("dom", "sub"), None, None),
        P(("dom", "sub"), None),
        P(("dom", "sub")),
        P(("dom", "sub"), None),
        P(("dom", "sub"), None, None),
        P(("dom", "sub"), None, None),
        P(("dom", "sub"), None, None),
        P(),
        P(("dom", "sub"), None),
        P(("dom", "sub"), None),
        P(("dom", "sub"), None, None),
    )
    out_specs = (P(("dom", "sub"), None), P(("dom", "sub"), None))
    return jax.shard_map(
        per_device, mesh=mesh, in_specs=in_specs, out_specs=out_specs, check_vma=False
    )
```

profile of v0, /device:TPU:1, one launch (start us, length us, event | category | flops | bytes accessed | tf_op | source)
XLA Modules:
  0.0 128.0 jit_solution(7954377808540108294)
XLA Ops:
  4.4 12.5 %collective-permute-start = (bf16[8,320]{1,0:T(8,128)(2,1)S(1)}, bf16[8,320]{1,0:T(8,128)(2,1)S(1)}, u32[]{:S(2)}, u32[]{:S(2)}) collective-permute-start(bf16[8,320]{1,0:T(8,128)(2,1)S(1)} %get-tuple-element.18), channel_id=1, source_target_pairs={{8,0},{10,2},{12,4},{14,6},{16,8},{18,10},{20,12},{22,14},{24,16},... | collective-permute-start | bytes 15368 | tf_op jit(solution)/shard_map/ppermute | solution.py:12
  16.9 4.2 %collective-permute-start.2 = (bf16[8,320]{1,0:T(8,128)(2,1)S(1)}, bf16[8,320]{1,0:T(8,128)(2,1)S(1)}, u32[]{:S(2)}, u32[]{:S(2)}) collective-permute-start(bf16[8,320]{1,0:T(8,128)(2,1)S(1)} %get-tuple-element.16), channel_id=1, source_target_pairs={{4,0},{6,2},{8,4},{10,6},{12,8},{14,10},{16,12},{18,14},{20,16},{2... | collective-permute-start | bytes 15368 | tf_op jit(solution)/shard_map/ppermute | solution.py:12
  25.5 7.3 %convolution_convert_fusion = bf16[16,320,400]{1,2,0:T(8,128)(2,1)S(1)} fusion(bf16[16,320,320]{2,1,0:T(8,128)(2,1)} %param.17, bf16[16,320,400]{1,2,0:T(8,128)(2,1)} %param.18), kind=kOutput, calls=%fused_computation.5 | convolution fusion | flops 1312768000 | bytes 11468800 | tf_op jit(solution)/shard_map/eab,ebc->eac/dot_general | solution.py:73
  32.9 2.0 %fusion = bf16[16,5,80,80]{2,3,1,0:T(8,128)(2,1)S(1)} fusion(bf16[16,320,5,80]{1,3,2,0:T(8,128)(2,1)S(1)} %bitcast.103, bf16[16,5,80,320]{3,2,1,0:T(8,128)(2,1)S(1)} %bitcast.102, f32[80,80]{0,1:T(8,128)S(1)} %copy.35, f32[16,5]{1,0:T(8,128)S(1)} %copy.34), kind=kOutput, calls=%fused_computation.4 | convolution fusion | flops 329216000 | bytes 9241920 | tf_op jit(solution)/shard_map/ejar,erjb->ejab/dot_general | solution.py:81
  36.2 2.4 %copy.36 = bf16[16,5,80,80]{3,2,1,0:T(8,128)(2,1)S(1)} copy(bf16[16,5,80,80]{2,3,1,0:T(8,128)(2,1)S(1)} %fusion) | data formatting | bytes 2048000 | tf_op jit(solution)/shard_map/convert_element_type | solution.py:85
  38.6 1.7 %reshape.127 = bf16[80,6400]{1,0:T(8,128)(2,1)S(1)} reshape(bf16[16,5,80,80]{3,2,1,0:T(8,128)(2,1)S(1)} %copy.36) | data formatting | bytes 2048000 | tf_op jit(solution)/shard_map/reshape | solution.py:92
  40.5 2.6 %collective-permute-start.6 = (bf16[8,320]{1,0:T(8,128)(2,1)S(1)}, bf16[8,320]{1,0:T(8,128)(2,1)S(1)}, u32[]{:S(2)}, u32[]{:S(2)}) collective-permute-start(bf16[8,320]{1,0:T(8,128)(2,1)S(1)} %get-tuple-element.11), channel_id=1, source_target_pairs={{250,0},{252,2},{254,4},{0,6},{2,8},{4,10},{6,12},{8,14},{10,16},{... | collective-permute-start | bytes 15368 | tf_op jit(solution)/shard_map/ppermute | solution.py:12
  43.1 3.5 %collective-permute-start.7 = (bf16[8,320]{1,0:T(8,128)(2,1)S(1)}, bf16[8,320]{1,0:T(8,128)(2,1)S(1)}, u32[]{:S(2)}, u32[]{:S(2)}) collective-permute-start(bf16[8,320]{1,0:T(8,128)(2,1)S(1)} %get-tuple-element.10), channel_id=1, source_target_pairs={{248,0},{250,2},{252,4},{254,6},{0,8},{2,10},{4,12},{6,14},{8,16},... | collective-permute-start | bytes 15368 | tf_op jit(solution)/shard_map/ppermute | solution.py:12
  46.6 2.7 %collective-permute-done.5 = bf16[8,320]{1,0:T(8,128)(2,1)S(1)} collective-permute-done((bf16[8,320]{1,0:T(8,128)(2,1)S(1)}, bf16[8,320]{1,0:T(8,128)(2,1)S(1)}, u32[]{:S(2)}, u32[]{:S(2)}) %collective-permute-start.5) | collective-permute-done | bytes 5152 | tf_op jit(solution)/shard_map/ppermute | solution.py:12
  50.5 3.2 %collective-permute-done.7 = bf16[8,320]{1,0:T(8,128)(2,1)S(1)} collective-permute-done((bf16[8,320]{1,0:T(8,128)(2,1)S(1)}, bf16[8,320]{1,0:T(8,128)(2,1)S(1)}, u32[]{:S(2)}, u32[]{:S(2)}) %collective-permute-start.7) | collective-permute-done | bytes 5152 | tf_op jit(solution)/shard_map/ppermute | solution.py:12
  54.8 3.3 %fusion.11 = bf16[16,1,320]{2,1,0:T(2,128)(2,1)S(1)} fusion(bf16[16,320,320]{2,1,0:T(8,128)(2,1)} %param.17, bf16[16,320,1]{1,0,2:T(8,128)(2,1)S(1)} %fusion.17), kind=kOutput, calls=%fused_computation.45 | convolution fusion | flops 3276800 | bytes 3297280 | tf_op jit(solution)/shard_map/eab,eb->ea/dot_general | solution.py:76
  58.1 4.6 %fusion.9 = f32[16,1,5,80]{3,1,2,0:T(1,128)S(1)} fusion(bf16[16,5,80,320]{3,2,1,0:T(8,128)(2,1)} %bitcast.99, bf16[16,320,1,1]{1,0,2,3:T(8,128)(2,1)S(1)} %bitcast.105), kind=kOutput, calls=%fused_computation.43 | convolution fusion | flops 4096000 | bytes 4131840 | tf_op jit(solution)/shard_map/ejar,er->eja/dot_general | solution.py:82
  62.9 1.3 gather_fusion.2
  65.5 2.8 %collective-permute-start.8 = (bf16[9,6480]{1,0:T(8,128)(2,1)S(1)}, bf16[9,6480]{1,0:T(8,128)(2,1)}, u32[]{:S(2)}, u32[]{:S(2)}) collective-permute-start(bf16[9,6480]{1,0:T(8,128)(2,1)S(1)} %get-tuple-element.9), channel_id=1, source_target_pairs={{8,0},{10,2},{12,4},{14,6},{16,8},{18,10},{20,12},{22,14},{24,16},... | collective-permute-start | bytes 349928 | tf_op jit(solution)/shard_map/ppermute | solution.py:12
  68.4 4.1 %collective-permute-start.10 = (bf16[9,6480]{1,0:T(8,128)(2,1)}, bf16[9,6480]{1,0:T(8,128)(2,1)S(1)}, u32[]{:S(2)}, u32[]{:S(2)}) collective-permute-start(bf16[9,6480]{1,0:T(8,128)(2,1)} %get-tuple-element.7), channel_id=1, source_target_pairs={{4,0},{6,2},{8,4},{10,6},{12,8},{14,10},{16,12},{18,14},{20,16},{2... | collective-permute-start | bytes 349928 | tf_op jit(solution)/shard_map/ppermute | solution.py:12
  72.7 1.3 collective-permute-start.12
  74.0 2.0 %collective-permute-done.8 = bf16[9,6480]{1,0:T(8,128)(2,1)} collective-permute-done((bf16[9,6480]{1,0:T(8,128)(2,1)S(1)}, bf16[9,6480]{1,0:T(8,128)(2,1)}, u32[]{:S(2)}, u32[]{:S(2)}) %collective-permute-start.8) | collective-permute-done | bytes 116672 | tf_op jit(solution)/shard_map/ppermute | solution.py:12
  75.9 3.5 %collective-permute-start.13 = (bf16[9,6480]{1,0:T(8,128)(2,1)}, bf16[9,6480]{1,0:T(8,128)(2,1)S(1)}, u32[]{:S(2)}, u32[]{:S(2)}) collective-permute-start(bf16[9,6480]{1,0:T(8,128)(2,1)} %get-tuple-element.4), channel_id=1, source_target_pairs={{252,0},{254,2},{0,4},{2,6},{4,8},{6,10},{8,12},{10,14},{12,16},{1... | collective-permute-start | bytes 349928 | tf_op jit(solution)/shard_map/ppermute | solution.py:12
  80.4 8.9 %collective-permute-done.9 = bf16[9,6480]{1,0:T(8,128)(2,1)S(1)} collective-permute-done((bf16[9,6480]{1,0:T(8,128)(2,1)}, bf16[9,6480]{1,0:T(8,128)(2,1)S(1)}, u32[]{:S(2)}, u32[]{:S(2)}) %collective-permute-start.9) | collective-permute-done | bytes 116672 | tf_op jit(solution)/shard_map/ppermute | solution.py:12
  89.3 7.5 %collective-permute-start.14 = (bf16[9,6480]{1,0:T(8,128)(2,1)S(1)}, bf16[9,6480]{1,0:T(8,128)(2,1)S(1)}, u32[]{:S(2)}, u32[]{:S(2)}) collective-permute-start(bf16[9,6480]{1,0:T(8,128)(2,1)S(1)} %get-tuple-element.3), channel_id=1, source_target_pairs={{250,0},{252,2},{254,4},{0,6},{2,8},{4,10},{6,12},{8,14},{10,16},{... | collective-permute-start | bytes 349928 | tf_op jit(solution)/shard_map/ppermute | solution.py:12
  96.8 3.3 %collective-permute-done.10 = bf16[9,6480]{1,0:T(8,128)(2,1)S(1)} collective-permute-done((bf16[9,6480]{1,0:T(8,128)(2,1)}, bf16[9,6480]{1,0:T(8,128)(2,1)S(1)}, u32[]{:S(2)}, u32[]{:S(2)}) %collective-permute-start.10) | collective-permute-done | bytes 116672 | tf_op jit(solution)/shard_map/ppermute | solution.py:12
  100.0 5.3 %collective-permute-start.15 = (bf16[9,6480]{1,0:T(8,128)(2,1)S(1)}, bf16[9,6480]{1,0:T(8,128)(2,1)S(1)}, u32[]{:S(2)}, u32[]{:S(2)}) collective-permute-start(bf16[9,6480]{1,0:T(8,128)(2,1)S(1)} %get-tuple-element.2), channel_id=1, source_target_pairs={{248,0},{250,2},{252,4},{254,6},{0,8},{2,10},{4,12},{6,14},{8,16},... | collective-permute-start | bytes 349928 | tf_op jit(solution)/shard_map/ppermute | solution.py:12
  106.1 6.5 %collective-permute-done.14 = bf16[9,6480]{1,0:T(8,128)(2,1)S(1)} collective-permute-done((bf16[9,6480]{1,0:T(8,128)(2,1)S(1)}, bf16[9,6480]{1,0:T(8,128)(2,1)S(1)}, u32[]{:S(2)}, u32[]{:S(2)}) %collective-permute-start.14) | collective-permute-done | bytes 116672 | tf_op jit(solution)/shard_map/ppermute | solution.py:12
  112.6 12.8 %collective-permute-done.15 = bf16[9,6480]{1,0:T(8,128)(2,1)S(1)} collective-permute-done((bf16[9,6480]{1,0:T(8,128)(2,1)S(1)}, bf16[9,6480]{1,0:T(8,128)(2,1)S(1)}, u32[]{:S(2)}, u32[]{:S(2)}) %collective-permute-start.15) | collective-permute-done | bytes 116672 | tf_op jit(solution)/shard_map/ppermute | solution.py:12
  (87 shorter events, 18.0 us)
Async XLA Ops:
  0.6 2.9 %copy-start = (bf16[16,320]{1,0:T(8,128)(2,1)S(1)}, bf16[16,320]{1,0:T(8,128)(2,1)}, u32[]{:S(2)}) copy-start(bf16[16,320]{1,0:T(8,128)(2,1)} %param.12) | copy-start | bytes 30724
  4.4 28.4 %slice-start = ((s8[4915200]{0:T(1024)(128)(4,1)}), s8[720896]{0:T(1024)(128)(4,1)S(1)}, s32[]{:S(2)}) async-start(s8[4915200]{0:T(1024)(128)(4,1)} %bitcast.100), calls=%async_computation | async-start | bytes 1441792
  4.4 30.6 %collective-permute-start = (bf16[8,320]{1,0:T(8,128)(2,1)S(1)}, bf16[8,320]{1,0:T(8,128)(2,1)S(1)}, u32[]{:S(2)}, u32[]{:S(2)}) collective-permute-start(bf16[8,320]{1,0:T(8,128)(2,1)S(1)} %get-tuple-element.18), channel_id=1, source_target_pairs={{8,0},{10,2},{12,4},{14,6},{16,8},{18,10},{20,12},{22,14},{24,16},... | collective-permute-start | bytes 15368 | tf_op jit(solution)/shard_map/ppermute | solution.py:12
  16.9 18.2 %collective-permute-start.1 = (bf16[8,320]{1,0:T(8,128)(2,1)S(1)}, bf16[8,320]{1,0:T(8,128)(2,1)S(1)}, u32[]{:S(2)}, u32[]{:S(2)}) collective-permute-start(bf16[8,320]{1,0:T(8,128)(2,1)S(1)} %get-tuple-element.17), channel_id=1, source_target_pairs={{6,0},{8,2},{10,4},{12,6},{14,8},{16,10},{18,12},{20,14},{22,16},{... | collective-permute-start | bytes 15368 | tf_op jit(solution)/shard_map/ppermute | solution.py:12
  16.9 18.2 %collective-permute-start.2 = (bf16[8,320]{1,0:T(8,128)(2,1)S(1)}, bf16[8,320]{1,0:T(8,128)(2,1)S(1)}, u32[]{:S(2)}, u32[]{:S(2)}) collective-permute-start(bf16[8,320]{1,0:T(8,128)(2,1)S(1)} %get-tuple-element.16), channel_id=1, source_target_pairs={{4,0},{6,2},{8,4},{10,6},{12,8},{14,10},{16,12},{18,14},{20,16},{2... | collective-permute-start | bytes 15368 | tf_op jit(solution)/shard_map/ppermute | solution.py:12
  21.1 14.0 %collective-permute-start.3 = (bf16[8,320]{1,0:T(8,128)(2,1)S(1)}, bf16[8,320]{1,0:T(8,128)(2,1)S(1)}, u32[]{:S(2)}, u32[]{:S(2)}) collective-permute-start(bf16[8,320]{1,0:T(8,128)(2,1)S(1)} %get-tuple-element.15), channel_id=1, source_target_pairs={{2,0},{4,2},{6,4},{8,6},{10,8},{12,10},{14,12},{16,14},{18,16},{20... | collective-permute-start | bytes 15368 | tf_op jit(solution)/shard_map/ppermute | solution.py:12
  25.5 7.3 %slice-start.1 = ((s8[4915200]{0:T(1024)(128)(4,1)}), s8[4194304]{0:T(1024)(128)(4,1)S(1)}, s32[]{:S(2)}) async-start(s8[4915200]{0:T(1024)(128)(4,1)} %bitcast.100), calls=%async_computation.1 | async-start | bytes 8388608
  35.1 11.5 %collective-permute-start.4 = (bf16[8,320]{1,0:T(8,128)(2,1)S(1)}, bf16[8,320]{1,0:T(8,128)(2,1)S(1)}, u32[]{:S(2)}, u32[]{:S(2)}) collective-permute-start(bf16[8,320]{1,0:T(8,128)(2,1)S(1)} %get-tuple-element.13), channel_id=1, source_target_pairs={{254,0},{0,2},{2,4},{4,6},{6,8},{8,10},{10,12},{12,14},{14,16},{16... | collective-permute-start | bytes 15368 | tf_op jit(solution)/shard_map/ppermute | solution.py:12
  40.4 8.9 %collective-permute-start.5 = (bf16[8,320]{1,0:T(8,128)(2,1)S(1)}, bf16[8,320]{1,0:T(8,128)(2,1)S(1)}, u32[]{:S(2)}, u32[]{:S(2)}) collective-permute-start(bf16[8,320]{1,0:T(8,128)(2,1)S(1)} %get-tuple-element.12), channel_id=1, source_target_pairs={{252,0},{254,2},{0,4},{2,6},{4,8},{6,10},{8,12},{10,14},{12,16},{1... | collective-permute-start | bytes 15368 | tf_op jit(solution)/shard_map/ppermute | solution.py:12
  40.5 10.0 %collective-permute-start.6 = (bf16[8,320]{1,0:T(8,128)(2,1)S(1)}, bf16[8,320]{1,0:T(8,128)(2,1)S(1)}, u32[]{:S(2)}, u32[]{:S(2)}) collective-permute-start(bf16[8,320]{1,0:T(8,128)(2,1)S(1)} %get-tuple-element.11), channel_id=1, source_target_pairs={{250,0},{252,2},{254,4},{0,6},{2,8},{4,10},{6,12},{8,14},{10,16},{... | collective-permute-start | bytes 15368 | tf_op jit(solution)/shard_map/ppermute | solution.py:12
  43.1 10.6 %collective-permute-start.7 = (bf16[8,320]{1,0:T(8,128)(2,1)S(1)}, bf16[8,320]{1,0:T(8,128)(2,1)S(1)}, u32[]{:S(2)}, u32[]{:S(2)}) collective-permute-start(bf16[8,320]{1,0:T(8,128)(2,1)S(1)} %get-tuple-element.10), channel_id=1, source_target_pairs={{248,0},{250,2},{252,4},{254,6},{0,8},{2,10},{4,12},{6,14},{8,16},... | collective-permute-start | bytes 15368 | tf_op jit(solution)/shard_map/ppermute | solution.py:12
  64.4 3.9 %copy-start.1 = (s32[1,9,9]{2,0,1:T(1,128)S(1)}, s32[1,9,9]{2,0,1:T(1,128)}, u32[]{:S(2)}) copy-start(s32[1,9,9]{2,0,1:T(1,128)} %param.23) | copy-start | bytes 976
  65.5 10.4 %collective-permute-start.8 = (bf16[9,6480]{1,0:T(8,128)(2,1)S(1)}, bf16[9,6480]{1,0:T(8,128)(2,1)}, u32[]{:S(2)}, u32[]{:S(2)}) collective-permute-start(bf16[9,6480]{1,0:T(8,128)(2,1)S(1)} %get-tuple-element.9), channel_id=1, source_target_pairs={{8,0},{10,2},{12,4},{14,6},{16,8},{18,10},{20,12},{22,14},{24,16},... | collective-permute-start | bytes 349928 | tf_op jit(solution)/shard_map/ppermute | solution.py:12
  68.4 20.9 %collective-permute-start.9 = (bf16[9,6480]{1,0:T(8,128)(2,1)}, bf16[9,6480]{1,0:T(8,128)(2,1)S(1)}, u32[]{:S(2)}, u32[]{:S(2)}) collective-permute-start(bf16[9,6480]{1,0:T(8,128)(2,1)} %get-tuple-element.8), channel_id=1, source_target_pairs={{6,0},{8,2},{10,4},{12,6},{14,8},{16,10},{18,12},{20,14},{22,16},{... | collective-permute-start | bytes 349928 | tf_op jit(solution)/shard_map/ppermute | solution.py:12
  68.4 31.6 %collective-permute-start.10 = (bf16[9,6480]{1,0:T(8,128)(2,1)}, bf16[9,6480]{1,0:T(8,128)(2,1)S(1)}, u32[]{:S(2)}, u32[]{:S(2)}) collective-permute-start(bf16[9,6480]{1,0:T(8,128)(2,1)} %get-tuple-element.7), channel_id=1, source_target_pairs={{4,0},{6,2},{8,4},{10,6},{12,8},{14,10},{16,12},{18,14},{20,16},{2... | collective-permute-start | bytes 349928 | tf_op jit(solution)/shard_map/ppermute | solution.py:12
  72.5 33.4 %collective-permute-start.11 = (bf16[9,6480]{1,0:T(8,128)(2,1)}, bf16[9,6480]{1,0:T(8,128)(2,1)S(1)}, u32[]{:S(2)}, u32[]{:S(2)}) collective-permute-start(bf16[9,6480]{1,0:T(8,128)(2,1)} %get-tuple-element.6), channel_id=1, source_target_pairs={{2,0},{4,2},{6,4},{8,6},{10,8},{12,10},{14,12},{16,14},{18,16},{20... | collective-permute-start | bytes 349928 | tf_op jit(solution)/shard_map/ppermute | solution.py:12
  72.7 33.3 %collective-permute-start.12 = (bf16[9,6480]{1,0:T(8,128)(2,1)}, bf16[9,6480]{1,0:T(8,128)(2,1)S(1)}, u32[]{:S(2)}, u32[]{:S(2)}) collective-permute-start(bf16[9,6480]{1,0:T(8,128)(2,1)} %get-tuple-element.5), channel_id=1, source_target_pairs={{254,0},{0,2},{2,4},{4,6},{6,8},{8,10},{10,12},{12,14},{14,16},{16... | collective-permute-start | bytes 349928 | tf_op jit(solution)/shard_map/ppermute | solution.py:12
  75.9 30.1 %collective-permute-start.13 = (bf16[9,6480]{1,0:T(8,128)(2,1)}, bf16[9,6480]{1,0:T(8,128)(2,1)S(1)}, u32[]{:S(2)}, u32[]{:S(2)}) collective-permute-start(bf16[9,6480]{1,0:T(8,128)(2,1)} %get-tuple-element.4), channel_id=1, source_target_pairs={{252,0},{254,2},{0,4},{2,6},{4,8},{6,10},{8,12},{10,14},{12,16},{1... | collective-permute-start | bytes 349928 | tf_op jit(solution)/shard_map/ppermute | solution.py:12
  89.3 23.3 %collective-permute-start.14 = (bf16[9,6480]{1,0:T(8,128)(2,1)S(1)}, bf16[9,6480]{1,0:T(8,128)(2,1)S(1)}, u32[]{:S(2)}, u32[]{:S(2)}) collective-permute-start(bf16[9,6480]{1,0:T(8,128)(2,1)S(1)} %get-tuple-element.3), channel_id=1, source_target_pairs={{250,0},{252,2},{254,4},{0,6},{2,8},{4,10},{6,12},{8,14},{10,16},{... | collective-permute-start | bytes 349928 | tf_op jit(solution)/shard_map/ppermute | solution.py:12
  100.0 25.3 %collective-permute-start.15 = (bf16[9,6480]{1,0:T(8,128)(2,1)S(1)}, bf16[9,6480]{1,0:T(8,128)(2,1)S(1)}, u32[]{:S(2)}, u32[]{:S(2)}) collective-permute-start(bf16[9,6480]{1,0:T(8,128)(2,1)S(1)} %get-tuple-element.2), channel_id=1, source_target_pairs={{248,0},{250,2},{252,4},{254,6},{0,8},{2,10},{4,12},{6,14},{8,16},... | collective-permute-start | bytes 349928 | tf_op jit(solution)/shard_map/ppermute | solution.py:12
where the time goes:
time: 128 us
  starting transfers between devices  49 us (38%)
  waiting for transfers between devices  41.1 us (32%)
  matrix products  17.8 us (14%)
  local copies, waits for them, and re-layouts  14.9 us (12%)
  other arithmetic  4.26 us (3%)
    ppermute x16, starting transfers between devices, passed_along(): return lax.ppermute(block, axis, route)  49 us
    ppermute x16, waiting for transfers between devices, passed_along(): return lax.ppermute(block, axis, route)  41.1 us
    dot_general x1, matrix products, per_device(): jnp.einsum('eab,ebc->eac', interior_inverse, inner_coupling, preferred_el...  7.3 us
    dot_general x1, matrix products, per_device(): jnp.einsum('ejar,er->eja', rows_in, interior_load, preferred_element_type...  4.59 us
    unnamed x26, local copies, waits for them, and re-layouts  3.6 us
    dot_general x1, matrix products, per_device(): jnp.einsum('eab,eb->ea', interior_inverse, projected, preferred_element_t...  3.3 us
    gather x4, local copies, waits for them, and re-layouts, pick_rows(): chosen = jnp.take(table, jnp.maximum(lookup, 0), axis=0)  2.72 us
  transfers between devices with their start and end apart: 16, of which 9 were waited for; matrix products, arithmetic and copies ran while one was open for 15% of the time, Pallas kernels for 0%

commit v1 on v0

v1 whole, which is shorter than its diff:
```python
import functools
import jax
import jax.numpy as jnp
from jax import lax
from jax.experimental import pallas as pl
from jax.experimental.pallas import tpu as pltpu
from jax.sharding import PartitionSpec as P

F32 = jnp.float32
BF16 = jnp.bfloat16
I32 = jnp.int32
NT = (((1,), (1,)), ((), ()))
TN = (((0,), (0,)), ((), ()))


def nt(a, b):
    return lax.dot_general(a, b, NT, preferred_element_type=F32)


def offset_at(k, reach):
    half = k // 2
    odd = k % 2
    return (1 - odd) * half + odd * (2 * reach - half)


def kernel(
    dims,
    states_hbm, send_hbm, slot_hbm, count_hbm, weight_hbm, inverse_hbm, inner_hbm, outer_hbm,
    mass_hbm, scale_hbm, shift_hbm, owner_hbm,
    schur_ref, rhs_ref,
    states, send_e, slot, count, weight, inverse, inner, outer, mass, scale, shift, owner,
    mapped, source_v, source_s, st_send, st_recv, il_ref, block32, flat32, wire, arrived,
    load32, load_wire, load_arrived, spread32,
    small_sem, source_sem, inverse_sem, inner_sem, outer_sem,
    st_ssem, st_rsem, w_ssem, w_rsem, l_ssem, l_rsem,
):
    reach, n_dom, n_elem, n_face, fu, ni, cap, capf, n_k = dims
    n_off = 2 * reach + 1
    owned = schur_ref.shape[0]
    flat_rows = capf * fu * fu // 128
    item_rows = fu * fu // 128
    me = lax.axis_index("dom")

    smalls = [
        pltpu.make_async_copy(a, b, small_sem.at[q])
        for q, (a, b) in enumerate([
            (shift_hbm, shift), (scale_hbm, scale), (mass_hbm, mass), (states_hbm, states),
            (send_hbm, send_e), (slot_hbm, slot), (count_hbm, count), (weight_hbm, weight),
            (owner_hbm, owner)])
    ]
    for c in smalls:
        c.start()

    def big(n):
        rows = pl.ds(n * n_face, n_face)
        return (
            pltpu.make_async_copy(inverse_hbm.at[n], inverse.at[n], inverse_sem.at[n]),
            pltpu.make_async_copy(inner_hbm.at[rows], inner.at[rows], inner_sem.at[n]),
            pltpu.make_async_copy(outer_hbm.at[rows], outer.at[rows], outer_sem.at[n]),
        )

    @pl.loop(0, n_elem)
    def _(n):
        a, b, _c = big(n)
        a.start()
        b.start()

    @pl.loop(0, n_elem)
    def _(n):
        big(n)[2].start()

    def partner(t):
        return {"dom": lax.rem(me + t - reach + n_dom, n_dom)}

    barrier = pltpu.get_barrier_semaphore()
    for t in range(n_off):
        if t != reach:
            pl.semaphore_signal(barrier, 1, device_id=partner(t), device_id_type=pl.DeviceIdType.MESH)

    smalls[0].wait()
    sh = shift[...]
    t3 = lax.broadcasted_iota(I32, (n_off, n_face, n_elem), 0) - reach
    j3 = lax.broadcasted_iota(I32, (n_off, n_face, n_elem), 1)
    n3 = lax.broadcasted_iota(I32, (n_off, n_face, n_elem), 2)
    hit = jnp.where(jnp.broadcast_to(sh[None], (n_off, n_face, n_elem)) == t3, 1, 0)
    per_elem = jnp.sum(hit, axis=1)
    lane = lax.broadcasted_iota(I32, (n_off, n_elem), 1)
    before = jnp.zeros((n_off, n_elem), I32)
    for n in range(n_elem - 1):
        before = before + jnp.where(lane > n, jnp.broadcast_to(per_elem[:, n:n + 1], (n_off, n_elem)), 0)
    rank = jnp.broadcast_to(before[:, None, :], (n_off, n_face, n_elem))
    for j in range(n_face - 1):
        rank = rank + jnp.where(j3 > j, jnp.broadcast_to(hit[:, j:j + 1, :], (n_off, n_face, n_elem)), 0)
    code = n3 * n_face + j3
    wide = lax.broadcasted_iota(I32, (n_off, 128), 1)
    table = jnp.zeros((n_off, 128), I32)
    for r in range(capf):
        found = jnp.sum(jnp.where((hit == 1) & (rank == r), code, 0), axis=1)
        total = jnp.sum(found, axis=1, keepdims=True)
        table = jnp.where(wide == r, jnp.broadcast_to(total, (n_off, 128)), table)
    source_v[0:n_off, :] = table
    source_copy = pltpu.make_async_copy(source_v, source_s, source_sem)
    source_copy.start()

    smalls[3].wait()
    smalls[4].wait()
    old = states[...]
    picks = send_e[...]
    e_row = lax.broadcasted_iota(I32, (n_elem, cap), 0)
    for t in range(n_off):
        sel = jnp.where(e_row == jnp.broadcast_to(picks[:, t:t + 1].reshape(1, cap), (n_elem, cap)), 1.0, 0.0)
        st_send[t] = lax.dot_general(sel.astype(BF16), old, TN, preferred_element_type=F32)

    pl.semaphore_wait(barrier, n_off - 1)

    def state_copy(t):
        return pltpu.make_async_remote_copy(
            src_ref=st_send.at[t], dst_ref=st_recv.at[t], send_sem=st_ssem.at[t], recv_sem=st_rsem.at[t],
            device_id=partner(t), device_id_type=pl.DeviceIdType.MESH)

    def wire_copy(t):
        return pltpu.make_async_remote_copy(
            src_ref=wire.at[t], dst_ref=arrived.at[t], send_sem=w_ssem.at[t], recv_sem=w_rsem.at[t],
            device_id=partner(t), device_id_type=pl.DeviceIdType.MESH)

    def load_copy(t):
        return pltpu.make_async_remote_copy(
            src_ref=load_wire.at[t], dst_ref=load_arrived.at[t], send_sem=l_ssem.at[t], recv_sem=l_rsem.at[t],
            device_id=partner(t), device_id_type=pl.DeviceIdType.MESH)

    for t in range(n_off):
        if t != reach:
            state_copy(t).start()

    @pl.loop(0, n_elem)
    def _(n):
        a, b, _c = big(n)
        a.wait()
        b.wait()
        rows = pl.ds(n * n_face, n_face)
        cols = inner[rows].reshape(n_face * fu, ni)
        mapped[rows] = nt(cols, inverse[n]).astype(BF16).reshape(n_face, fu, ni)

    @pl.loop(0, n_elem)
    def _(n):
        big(n)[2].wait()

    smalls[1].wait()
    smalls[2].wait()
    source_copy.wait()
    flat32[flat_rows:, :] = jnp.zeros((flat32.shape[0] - flat_rows, 128), F32)
    load32[...] = jnp.zeros_like(load32)

    groups = capf * fu // 8
    out_rows = 8 * fu // 128

    @pl.loop(0, n_off)
    def _(k):
        t = offset_at(k, reach)
        face = mass[...]
        for r in range(capf):
            i = source_s[t, r]
            corr = nt(outer[i], mapped[i])
            block32[pl.ds(r * fu, fu), 0:fu] = scale[i % n_face, i // n_face] * face - corr
        lane_of = lax.broadcasted_iota(I32, (groups, 128), 1)
        turned = []
        for s in range(8):
            part = block32[pl.ds(s, groups, stride=8), :]
            by = (s * fu) % 128
            turned.append(pltpu.roll(part, by, 1) if by else part)
        for m in range(out_rows):
            lo, hi = m * 128, m * 128 + 128
            segs = [s for s in range(8) if s * fu < hi and (s + 1) * fu > lo]
            row = turned[segs[-1]]
            for s in reversed(segs[:-1]):
                row = jnp.where(lane_of < (s + 1) * fu - lo, turned[s], row)
            flat32[pl.ds(m, groups, stride=out_rows), :] = row
        wire[t] = flat32[...].astype(BF16)

        @pl.when(k < n_off - 1)
        def _():
            wire_copy(t).start()

    for q in (5, 6, 7, 8):
        smalls[q].wait()
    st_recv[reach] = st_send[reach]
    for t in range(n_off):
        if t != reach:
            state_copy(t).wait()
    n_slot = n_off * cap
    q_row = lax.broadcasted_iota(I32, (n_slot, n_elem), 0)
    mix = jnp.zeros((n_slot, n_elem), F32)
    live = count[...]
    for k in range(n_k):
        w = jnp.where(live > k, weight[k:k + 1, :], 0.0)
        at = jnp.broadcast_to(slot[k:k + 1, :], (n_slot, n_elem)) == q_row
        mix = mix + jnp.where(at, jnp.broadcast_to(w, (n_slot, n_elem)), 0.0)
    mix_t = jnp.transpose(mix)
    gathered = st_recv[...].reshape(n_slot, ni)
    top = jnp.dot(mix_t, gathered, precision=lax.Precision.HIGHEST, preferred_element_type=F32)
    projected = (top / jnp.sum(mix_t, axis=1, keepdims=True)).astype(BF16)
    row_of = lax.broadcasted_iota(I32, (n_elem, ni), 0)
    il_ref[...] = jnp.zeros_like(il_ref)

    @pl.loop(0, n_elem)
    def _(n):
        il_ref[...] += jnp.where(row_of == n, nt(projected, inverse[n]), 0.0)

    @pl.loop(0, n_off)
    def _(k):
        t = offset_at(k, reach)
        for r in range(capf):
            i = source_s[t, r]
            il = il_ref[pl.ds(i // n_face, 1), :].astype(BF16)
            load32[r:r + 1, 0:fu] = -nt(il, outer[i])
        load_wire[t] = load32[...].astype(BF16)

        @pl.when(k < n_off - 1)
        def _():
            load_copy(t).start()

    schur_ref[...] = jnp.zeros_like(schur_ref)
    rhs_ref[...] = jnp.zeros_like(rhs_ref)
    f_row = lax.broadcasted_iota(I32, (owned, capf), 0)
    arrived[reach] = wire[reach]
    load_arrived[reach] = load_wire[reach]
    chunk = 5

    def add_up(t):
        names = jnp.where(f_row == jnp.broadcast_to(owner[t], (owned, capf)), 1.0, 0.0).astype(BF16)
        spread32[...] = arrived[t].astype(F32)
        for b in range(0, item_rows, chunk):
            rows = jnp.concatenate(
                [spread32[pl.ds(b + d, capf, stride=item_rows), :] for d in range(chunk)], axis=1).astype(BF16)
            schur_ref[:, b * 128:(b + chunk) * 128] += jnp.dot(names, rows, preferred_element_type=F32)
        loads = load_arrived[t].astype(F32)[0:capf, 0:fu].astype(BF16)
        rhs_ref[...] += jnp.dot(names, loads, preferred_element_type=F32)

    add_up(reach)

    @pl.loop(0, n_off - 1)
    def _(k):
        t = offset_at(k, reach)
        wire_copy(t).wait_recv()
        load_copy(t).wait_recv()
        add_up(t)

    @pl.loop(0, n_off - 1)
    def _(k):
        t = offset_at(k, reach)
        wire_copy(t).wait_send()
        load_copy(t).wait_send()


def per_device(
    n_dom,
    old_states, send_elem, recv_slot, intersection_count, intersection_weight, interior_inverse,
    inner_coupling, face_coupling, face_mass, face_scale, face_shift, owner_row,
):
    n_elem, ni = old_states.shape
    n_off, cap = send_elem.shape[1:]
    capf = owner_row.shape[2]
    n_face = face_scale.shape[1]
    fu = face_mass.shape[0]
    n_k = recv_slot.shape[1]
    reach = (n_off - 1) // 2
    items = n_elem * n_face
    owned = items // 2
    wire_rows = -(-(capf * fu * fu // 128) // 16) * 16
    ins = (
        old_states,
        jnp.swapaxes(send_elem, 1, 2)[0],
        recv_slot.T,
        intersection_count.reshape(1, n_elem),
        intersection_weight.T,
        interior_inverse,
        jnp.swapaxes(inner_coupling, 1, 2).reshape(items, fu, ni),
        face_coupling.reshape(items, fu, ni),
        face_mass,
        face_scale.T,
        face_shift.T,
        jnp.swapaxes(owner_row, 0, 1),
    )
    scratch = []
    for q, a in enumerate(ins):
        space = pltpu.SMEM if q == 9 else pltpu.VMEM
        scratch.append(space(a.shape, a.dtype))
    dma = pltpu.SemaphoreType.DMA
    scratch += [
        pltpu.VMEM((items, fu, ni), BF16),
        pltpu.VMEM((16, 128), I32),
        pltpu.SMEM((16, 128), I32),
        pltpu.VMEM((n_off, cap, ni), F32),
        pltpu.VMEM((n_off, cap, ni), F32),
        pltpu.VMEM((n_elem, ni), F32),
        pltpu.VMEM((capf * fu, 128), F32),
        pltpu.VMEM((wire_rows, 128), F32),
        pltpu.VMEM((n_off, wire_rows, 128), BF16),
        pltpu.VMEM((n_off, wire_rows, 128), BF16),
        pltpu.VMEM((16, 128), F32),
        pltpu.VMEM((n_off, 16, 128), BF16),
        pltpu.VMEM((n_off, 16, 128), BF16),
        pltpu.VMEM((wire_rows, 128), F32),
        dma((9,)),
        dma(()),
        dma((n_elem,)),
        dma((n_elem,)),
        dma((n_elem,)),
    ] + [dma((n_off,)) for _ in range(6)]
    dims = (reach, n_dom, n_elem, n_face, fu, ni, cap, capf, n_k)
    return pl.pallas_call(
        functools.partial(kernel, dims),
        out_shape=(
            jax.ShapeDtypeStruct((owned, fu * fu), F32),
            jax.ShapeDtypeStruct((owned, fu), F32),
        ),
        in_specs=[pl.BlockSpec(memory_space=pl.ANY)] * len(ins),
        out_specs=(pl.BlockSpec(memory_space=pltpu.VMEM), pl.BlockSpec(memory_space=pltpu.VMEM)),
        scratch_shapes=scratch,
        compiler_params=pltpu.CompilerParams(
            collective_id=0, has_side_effects=True, vmem_limit_bytes=56 * 1024 * 1024),
        name="condense",
    )(*ins)


def solution(mesh):
    part = P(("dom", "sub"))
    in_specs = (part,) * 8 + (P(),) + (part,) * 3
    return jax.shard_map(
        functools.partial(per_device, mesh.shape["dom"]),
        mesh=mesh, in_specs=in_specs, out_specs=(part, part), check_vma=False)
```

time: 128 us -> 56.5 us (0.44)
  Pallas kernels: 0 us -> 52.1 us
  starting transfers between devices: 49 us -> 0 us
  waiting for transfers between devices: 41.1 us -> 0 us
  matrix products: 17.8 us -> 0 us
  local copies, waits for them, and re-layouts: 14.9 us -> 3.57 us
  other arithmetic: 4.26 us -> 0 us
    pallas_call x0 -> x1, Pallas kernels: none -> 52.1 us  [per_device(): pl.pallas_call(functools.partial(kernel, dims), out_shape=(jax.ShapeDtype...]
    ppermute x16 -> x0, starting transfers between devices: 49 us -> none  [passed_along(): return lax.ppermute(block, axis, route)]
    ppermute x16 -> x0, waiting for transfers between devices: 41.1 us -> none  [passed_along(): return lax.ppermute(block, axis, route)]
    dot_general x6 -> x0, matrix products: 17.8 us -> none  [the longest x1 7.3 us: per_device(): jnp.einsum('eab,ebc->eac', interior_inverse, inner_coupling, preferred_el...]
    slice x3 -> x0, local copies, waits for them, and re-layouts: 2.76 us -> none  [the longest x1 1.13 us: per_device(): pieces.append(passed_along(packed[offset], 'dom', offset - max_shift))]
    gather x4 -> x0, local copies, waits for them, and re-layouts: 2.72 us -> none  [pick_rows(): chosen = jnp.take(table, jnp.maximum(lookup, 0), axis=0)]
    reshape x4 -> x0, local copies, waits for them, and re-layouts: 2.5 us -> none  [the longest x1 1.75 us: per_device(): schur_block.reshape(item_count, face_size * face_size)]
    convert_element_type x1 -> x0, local copies, waits for them, and re-layouts: 2.4 us -> none  [per_device(): (face_scale[:, :, None, None] * face_mass[None, None] - correction).astyp...]
  transfers between devices with their start and end apart: 16 -> 0, of which waited for: 9 -> 0; matrix products, arithmetic and copies ran while one was open for 15% -> 0% of each run, Pallas kernels for 0% -> 0%
where the time goes in v1:
time: 56.5 us; the launch traced here: 56.3 us
  Pallas kernels  52.1 us (92%)
  local copies, waits for them, and re-layouts  3.57 us (6%)
  between operations  0.64 us (1%)
    pallas_call x1, Pallas kernels, per_device(): pl.pallas_call(functools.partial(kernel, dims), out_shape=(jax.ShapeDtype...  52.1 us
    unnamed x2, local copies, waits for them, and re-layouts  3.57 us

profile of v1, /device:TPU:1, one launch (start us, length us, event | category | flops | bytes accessed | tf_op | source)
XLA Modules:
  0.0 56.3 jit_solution(5942501769012417346)
XLA Ops:
  0.6 52.1 %condense.1 = (f32[40,6400]{1,0:T(8,128)}, f32[40,80]{1,0:T(8,128)}) custom-call(bf16[16,320]{1,0:T(8,128)(2,1)} %states_hbm.1, s32[8,9]{1,0:T(8,128)} %bitcast.16, s32[4,16]{1,0:T(4,128)} %bitcast.19, s32[1,16]{1,0:T(1,128)} %bitcast.21, f32[4,16]{1,0:T(4,128)} %bitcast.20, bf16[16,320,320]{2,1,0:T(8,128)(2,1)} %inverse_hbm.1, ...), custom_call_target="tpu_custom_call" | custom-call | tf_op jit(solution)/shard_map/condense/pallas_call | solution.py:311
  52.7 2.2 %copy.16 = f32[40,6400]{1,0:T(8,128)} copy(f32[40,6400]{1,0:T(8,128)} %get-tuple-element.4) | data formatting | bytes 2048000
  54.9 1.3 %copy.17 = f32[40,80]{1,0:T(8,128)} copy(f32[40,80]{1,0:T(8,128)} %get-tuple-element.5) | data formatting | bytes 25600

commit v2 on v1

--- a/solution.py
+++ b/solution.py
@@ -18,9 +18,15 @@
 
 
 def offset_at(k, reach):
-    half = k // 2
-    odd = k % 2
-    return (1 - odd) * half + odd * (2 * reach - half)
+    pair = k // 2
+    far = reach - pair // 2
+    near = (pair + 1) // 2
+    size = (1 - pair % 2) * far + (pair % 2) * near
+    return reach + size * (1 - 2 * (k % 2))
+
+
+def near_first(k, reach):
+    return reach + (k // 2 + 1) * (1 - 2 * (k % 2))
 
 
 def kernel(
@@ -51,23 +57,25 @@
     for c in smalls:
         c.start()
 
-    def big(n):
+    def load_inverse(n):
+        return pltpu.make_async_copy(inverse_hbm.at[n], inverse.at[n], inverse_sem.at[n])
+
+    def load_inner(n):
         rows = pl.ds(n * n_face, n_face)
-        return (
-            pltpu.make_async_copy(inverse_hbm.at[n], inverse.at[n], inverse_sem.at[n]),
-            pltpu.make_async_copy(inner_hbm.at[rows], inner.at[rows], inner_sem.at[n]),
-            pltpu.make_async_copy(outer_hbm.at[rows], outer.at[rows], outer_sem.at[n]),
-        )
+        return pltpu.make_async_copy(inner_hbm.at[rows], inner.at[rows], inner_sem.at[n])
+
+    def load_outer(n):
+        rows = pl.ds(n * n_face, n_face)
+        return pltpu.make_async_copy(outer_hbm.at[rows], outer.at[rows], outer_sem.at[n])
 
     @pl.loop(0, n_elem)
     def _(n):
-        a, b, _c = big(n)
-        a.start()
-        b.start()
+        load_inverse(n).start()
+        load_inner(n).start()
 
     @pl.loop(0, n_elem)
     def _(n):
-        big(n)[2].start()
+        load_outer(n).start()
 
     def partner(t):
         return {"dom": lax.rem(me + t - reach + n_dom, n_dom)}
@@ -77,7 +85,21 @@
         if t != reach:
             pl.semaphore_signal(barrier, 1, device_id=partner(t), device_id_type=pl.DeviceIdType.MESH)
 
+    def map_group(lo, hi):
+        for n in range(lo, hi):
+            load_inverse(n).wait()
+            load_inner(n).wait()
+        for n in range(lo, hi):
+            rows = slice(n * n_face, (n + 1) * n_face)
+            cols = inner[rows].reshape(n_face * fu, ni)
+            mapped[rows] = nt(cols, inverse[n]).astype(BF16).reshape(n_face, fu, ni)
+
+    starts = [0, n_elem // 8, n_elem // 4, n_elem // 2, 3 * n_elem // 4, n_elem]
     smalls[0].wait()
+    smalls[3].wait()
+    smalls[4].wait()
+    map_group(starts[0], starts[1])
+
     sh = shift[...]
     t3 = lax.broadcasted_iota(I32, (n_off, n_face, n_elem), 0) - reach
     j3 = lax.broadcasted_iota(I32, (n_off, n_face, n_elem), 1)
@@ -102,8 +124,6 @@
     source_copy = pltpu.make_async_copy(source_v, source_s, source_sem)
     source_copy.start()
 
-    smalls[3].wait()
-    smalls[4].wait()
     old = states[...]
     picks = send_e[...]
     e_row = lax.broadcasted_iota(I32, (n_elem, cap), 0)
@@ -132,18 +152,12 @@
         if t != reach:
             state_copy(t).start()
 
+    for lo, hi in zip(starts[1:-1], starts[2:]):
+        map_group(lo, hi)
+
     @pl.loop(0, n_elem)
     def _(n):
-        a, b, _c = big(n)
-        a.wait()
-        b.wait()
-        rows = pl.ds(n * n_face, n_face)
-        cols = inner[rows].reshape(n_face * fu, ni)
-        mapped[rows] = nt(cols, inverse[n]).astype(BF16).reshape(n_face, fu, ni)
-
-    @pl.loop(0, n_elem)
-    def _(n):
-        big(n)[2].wait()
+        load_outer(n).wait()
 
     smalls[1].wait()
     smalls[2].wait()
@@ -154,9 +168,7 @@
     groups = capf * fu // 8
     out_rows = 8 * fu // 128
 
-    @pl.loop(0, n_off)
-    def _(k):
-        t = offset_at(k, reach)
+    def pack(t):
         face = mass[...]
         for r in range(capf):
             i = source_s[t, r]
@@ -177,9 +189,13 @@
             flat32[pl.ds(m, groups, stride=out_rows), :] = row
         wire[t] = flat32[...].astype(BF16)
 
-        @pl.when(k < n_off - 1)
-        def _():
-            wire_copy(t).start()
+    @pl.loop(0, n_off - 1)
+    def _(k):
+        t = offset_at(k, reach)
+        pack(t)
+        wire_copy(t).start()
+
+    pack(reach)
 
     for q in (5, 6, 7, 8):
         smalls[q].wait()
@@ -206,48 +222,61 @@
     def _(n):
         il_ref[...] += jnp.where(row_of == n, nt(projected, inverse[n]), 0.0)
 
-    @pl.loop(0, n_off)
-    def _(k):
-        t = offset_at(k, reach)
+    def pack_loads(t):
         for r in range(capf):
             i = source_s[t, r]
             il = il_ref[pl.ds(i // n_face, 1), :].astype(BF16)
             load32[r:r + 1, 0:fu] = -nt(il, outer[i])
         load_wire[t] = load32[...].astype(BF16)
 
-        @pl.when(k < n_off - 1)
-        def _():
-            load_copy(t).start()
-
-    schur_ref[...] = jnp.zeros_like(schur_ref)
-    rhs_ref[...] = jnp.zeros_like(rhs_ref)
+    @pl.loop(0, n_off - 1)
+    def _(k):
+        t = offset_at(k, reach)
+        pack_loads(t)
+        load_copy(t).start()
+
+    pack_loads(reach)
+
     f_row = lax.broadcasted_iota(I32, (owned, capf), 0)
-    arrived[reach] = wire[reach]
-    load_arrived[reach] = load_wire[reach]
     chunk = 5
 
-    def add_up(t):
-        names = jnp.where(f_row == jnp.broadcast_to(owner[t], (owned, capf)), 1.0, 0.0).astype(BF16)
-        spread32[...] = arrived[t].astype(F32)
+    def names(t):
+        hits = f_row == jnp.broadcast_to(owner[t], (owned, capf))
+        return jnp.where(hits, 1.0, 0.0).astype(BF16)
+
+    def add_up(t, received, first):
+        who = names(t)
+        spread32[...] = received.astype(F32)
         for b in range(0, item_rows, chunk):
             rows = jnp.concatenate(
                 [spread32[pl.ds(b + d, capf, stride=item_rows), :] for d in range(chunk)], axis=1).astype(BF16)
-            schur_ref[:, b * 128:(b + chunk) * 128] += jnp.dot(names, rows, preferred_element_type=F32)
+            part = jnp.dot(who, rows, preferred_element_type=F32)
+            cols = slice(b * 128, (b + chunk) * 128)
+            schur_ref[:, cols] = part if first else schur_ref[:, cols] + part
+
+    add_up(reach, wire[reach], True)
+
+    @pl.loop(0, n_off - 1)
+    def _(k):
+        t = near_first(k, reach)
+        wire_copy(t).wait_recv()
+        add_up(t, arrived[t], False)
+
+    @pl.loop(0, n_off - 1)
+    def _(k):
+        t = near_first(k, reach)
+        load_copy(t).wait_recv()
+
+    load_arrived[reach] = load_wire[reach]
+    rhs = jnp.zeros(rhs_ref.shape, F32)
+    for t in range(n_off):
         loads = load_arrived[t].astype(F32)[0:capf, 0:fu].astype(BF16)
-        rhs_ref[...] += jnp.dot(names, loads, preferred_element_type=F32)
-
-    add_up(reach)
-
-    @pl.loop(0, n_off - 1)
-    def _(k):
-        t = offset_at(k, reach)
-        wire_copy(t).wait_recv()
-        load_copy(t).wait_recv()
-        add_up(t)
-
-    @pl.loop(0, n_off - 1)
-    def _(k):
-        t = offset_at(k, reach)
+        rhs = rhs + jnp.dot(names(t), loads, preferred_element_type=F32)
+    rhs_ref[...] = rhs
+
+    @pl.loop(0, n_off - 1)
+    def _(k):
+        t = near_first(k, reach)
         wire_copy(t).wait_send()
         load_copy(t).wait_send()
 
@@ -308,19 +337,20 @@
         dma((n_elem,)),
     ] + [dma((n_off,)) for _ in range(6)]
     dims = (reach, n_dom, n_elem, n_face, fu, ni, cap, capf, n_k)
-    return pl.pallas_call(
+    sums = pl.pallas_call(
         functools.partial(kernel, dims),
         out_shape=(
             jax.ShapeDtypeStruct((owned, fu * fu), F32),
             jax.ShapeDtypeStruct((owned, fu), F32),
         ),
-        in_specs=[pl.BlockSpec(memory_space=pl.ANY)] * len(ins),
+        in_specs=[pl.BlockSpec(memory_space=pltpu.HBM)] * len(ins),
         out_specs=(pl.BlockSpec(memory_space=pltpu.VMEM), pl.BlockSpec(memory_space=pltpu.VMEM)),
         scratch_shapes=scratch,
         compiler_params=pltpu.CompilerParams(
-            collective_id=0, has_side_effects=True, vmem_limit_bytes=56 * 1024 * 1024),
+            collective_id=0, has_side_effects=True, vmem_limit_bytes=52 * 1024 * 1024),
         name="condense",
-    )(*ins)
+    )(*[pltpu.with_memory_space_constraint(a, pltpu.HBM) for a in ins])
+    return sums
 
 
 def solution(mesh):

time: 56.5 us -> 49.7 us (0.88)
  Pallas kernels: 52.1 us -> 47.4 us
  local copies, waits for them, and re-layouts: 3.57 us -> 1.57 us
    pallas_call x1, Pallas kernels: 52.1 us -> 47.4 us  [per_device(): pl.pallas_call(functools.partial(kernel, dims), out_shape=(jax.ShapeDtype...]
    unnamed x2, local copies, waits for them, and re-layouts: 3.57 us -> 1.57 us
where the time goes in v2:
time: 49.7 us; the launch traced here: 49.6 us
  Pallas kernels  47.4 us (95%)
  local copies, waits for them, and re-layouts  1.57 us (3%)
  between operations  0.64 us (1%)
    pallas_call x1, Pallas kernels, per_device(): pl.pallas_call(functools.partial(kernel, dims), out_shape=(jax.ShapeDtype...  47.4 us
    unnamed x2, local copies, waits for them, and re-layouts  1.57 us

profile of v2, /device:TPU:1, one launch (start us, length us, event | category | flops | bytes accessed | tf_op | source)
XLA Modules:
  0.0 49.6 jit_solution(4178698644789404932)
XLA Ops:
  0.6 47.4 %condense.1 = (f32[40,6400]{1,0:T(8,128)S(1)}, f32[40,80]{1,0:T(8,128)S(1)}) custom-call(bf16[16,320]{1,0:T(8,128)(2,1)} %states_hbm.1, s32[8,9]{1,0:T(8,128)} %bitcast.16, s32[4,16]{1,0:T(4,128)} %bitcast.19, s32[1,16]{1,0:T(1,128)} %bitcast.21, f32[4,16]{1,0:T(4,128)} %bitcast.20, bf16[16,320,320]{2,1,0:T(8,128)(2,1)} %inverse_hbm.1, ...), custom_call_target="tpu_custom_call" | custom-call | tf_op jit(solution)/shard_map/condense/pallas_call | solution.py:340
  48.1 1.0 %copy.16 = f32[40,6400]{1,0:T(8,128)} copy(f32[40,6400]{1,0:T(8,128)S(1)} %get-tuple-element.4) | data formatting | bytes 2048000
  49.0 0.6 %copy.17 = f32[40,80]{1,0:T(8,128)} copy(f32[40,80]{1,0:T(8,128)S(1)} %get-tuple-element.5) | data formatting | bytes 25600

commit v3 on v2

--- a/solution.py
+++ b/solution.py
@@ -17,16 +17,17 @@
     return lax.dot_general(a, b, NT, preferred_element_type=F32)
 
 
-def offset_at(k, reach):
-    pair = k // 2
-    far = reach - pair // 2
-    near = (pair + 1) // 2
-    size = (1 - pair % 2) * far + (pair % 2) * near
-    return reach + size * (1 - 2 * (k % 2))
-
-
-def near_first(k, reach):
-    return reach + (k // 2 + 1) * (1 - 2 * (k % 2))
+def offset_at(k, reach, low):
+    back = k // reach
+    size = reach - (k - back * reach)
+    return reach + (1 - 2 * low) * (1 - 2 * back) * size
+
+
+def arrival_at(k, reach, low):
+    back = k // reach
+    size = k - back * reach + 1
+    sign = (1 - 2 * low) * (1 - 2 * back)
+    return reach + sign * size
 
 
 def kernel(
@@ -36,16 +37,18 @@
     schur_ref, rhs_ref,
     states, send_e, slot, count, weight, inverse, inner, outer, mass, scale, shift, owner,
     mapped, source_v, source_s, st_send, st_recv, il_ref, block32, flat32, wire, arrived,
-    load32, load_wire, load_arrived, spread32,
+    tail32, load_wire, load_arrived, spread32,
     small_sem, source_sem, inverse_sem, inner_sem, outer_sem,
     st_ssem, st_rsem, w_ssem, w_rsem, l_ssem, l_rsem,
 ):
     reach, n_dom, n_elem, n_face, fu, ni, cap, capf, n_k = dims
     n_off = 2 * reach + 1
     owned = schur_ref.shape[0]
-    flat_rows = capf * fu * fu // 128
     item_rows = fu * fu // 128
+    wire_rows = wire.shape[1]
+    rest = capf * item_rows - wire_rows
     me = lax.axis_index("dom")
+    low = 1 - lax.rem(me, 2 * reach) // reach
 
     smalls = [
         pltpu.make_async_copy(a, b, small_sem.at[q])
@@ -54,28 +57,31 @@
             (send_hbm, send_e), (slot_hbm, slot), (count_hbm, count), (weight_hbm, weight),
             (owner_hbm, owner)])
     ]
-    for c in smalls:
-        c.start()
-
-    def load_inverse(n):
-        return pltpu.make_async_copy(inverse_hbm.at[n], inverse.at[n], inverse_sem.at[n])
-
-    def load_inner(n):
-        rows = pl.ds(n * n_face, n_face)
-        return pltpu.make_async_copy(inner_hbm.at[rows], inner.at[rows], inner_sem.at[n])
-
-    def load_outer(n):
-        rows = pl.ds(n * n_face, n_face)
-        return pltpu.make_async_copy(outer_hbm.at[rows], outer.at[rows], outer_sem.at[n])
-
-    @pl.loop(0, n_elem)
-    def _(n):
-        load_inverse(n).start()
-        load_inner(n).start()
-
-    @pl.loop(0, n_elem)
-    def _(n):
-        load_outer(n).start()
+    starts = [0, n_elem // 8, n_elem // 4, n_elem // 2, 3 * n_elem // 4, n_elem]
+    groups_of = list(zip(starts[:-1], starts[1:]))
+
+    def load_group(g):
+        lo, hi = groups_of[g]
+        rows = pl.ds(lo * n_face, (hi - lo) * n_face)
+        return (
+            pltpu.make_async_copy(inverse_hbm.at[pl.ds(lo, hi - lo)], inverse.at[pl.ds(lo, hi - lo)], inverse_sem.at[g]),
+            pltpu.make_async_copy(inner_hbm.at[rows], inner.at[rows], inner_sem.at[g]),
+        )
+
+    def load_outer(h):
+        rows = pl.ds(h * n_elem * n_face // 2, n_elem * n_face // 2)
+        return pltpu.make_async_copy(outer_hbm.at[rows], outer.at[rows], outer_sem.at[h])
+
+    def start(*copies):
+        for c in copies:
+            c.start()
+
+    start(*load_group(0))
+    start(smalls[0], smalls[3], smalls[4])
+    for g in range(1, len(groups_of)):
+        start(*load_group(g))
+    start(load_outer(0), load_outer(1))
+    start(*(smalls[q] for q in (1, 2, 5, 6, 7, 8)))
 
     def partner(t):
         return {"dom": lax.rem(me + t - reach + n_dom, n_dom)}
@@ -85,20 +91,18 @@
         if t != reach:
             pl.semaphore_signal(barrier, 1, device_id=partner(t), device_id_type=pl.DeviceIdType.MESH)
 
-    def map_group(lo, hi):
-        for n in range(lo, hi):
-            load_inverse(n).wait()
-            load_inner(n).wait()
-        for n in range(lo, hi):
+    def map_group(g):
+        for c in load_group(g):
+            c.wait()
+        for n in range(*groups_of[g]):
             rows = slice(n * n_face, (n + 1) * n_face)
             cols = inner[rows].reshape(n_face * fu, ni)
             mapped[rows] = nt(cols, inverse[n]).astype(BF16).reshape(n_face, fu, ni)
 
-    starts = [0, n_elem // 8, n_elem // 4, n_elem // 2, 3 * n_elem // 4, n_elem]
     smalls[0].wait()
     smalls[3].wait()
     smalls[4].wait()
-    map_group(starts[0], starts[1])
+    map_group(0)
 
     sh = shift[...]
     t3 = lax.broadcasted_iota(I32, (n_off, n_face, n_elem), 0) - reach
@@ -131,8 +135,6 @@
         sel = jnp.where(e_row == jnp.broadcast_to(picks[:, t:t + 1].reshape(1, cap), (n_elem, cap)), 1.0, 0.0)
         st_send[t] = lax.dot_general(sel.astype(BF16), old, TN, preferred_element_type=F32)
 
-    pl.semaphore_wait(barrier, n_off - 1)
-
     def state_copy(t):
         return pltpu.make_async_remote_copy(
             src_ref=st_send.at[t], dst_ref=st_recv.at[t], send_sem=st_ssem.at[t], recv_sem=st_rsem.at[t],
@@ -148,22 +150,15 @@
             src_ref=load_wire.at[t], dst_ref=load_arrived.at[t], send_sem=l_ssem.at[t], recv_sem=l_rsem.at[t],
             device_id=partner(t), device_id_type=pl.DeviceIdType.MESH)
 
-    for t in range(n_off):
-        if t != reach:
-            state_copy(t).start()
-
-    for lo, hi in zip(starts[1:-1], starts[2:]):
-        map_group(lo, hi)
-
-    @pl.loop(0, n_elem)
-    def _(n):
-        load_outer(n).wait()
-
+    for g in range(1, len(groups_of)):
+        map_group(g)
+    load_outer(0).wait()
+    load_outer(1).wait()
     smalls[1].wait()
     smalls[2].wait()
     source_copy.wait()
-    flat32[flat_rows:, :] = jnp.zeros((flat32.shape[0] - flat_rows, 128), F32)
-    load32[...] = jnp.zeros_like(load32)
+    tail32[...] = jnp.zeros_like(tail32)
+    spread32[wire_rows:, :] = jnp.zeros((spread32.shape[0] - wire_rows, 128), F32)
 
     groups = capf * fu // 8
     out_rows = 8 * fu // 128
@@ -187,11 +182,19 @@
             for s in reversed(segs[:-1]):
                 row = jnp.where(lane_of < (s + 1) * fu - lo, turned[s], row)
             flat32[pl.ds(m, groups, stride=out_rows), :] = row
-        wire[t] = flat32[...].astype(BF16)
-
-    @pl.loop(0, n_off - 1)
-    def _(k):
-        t = offset_at(k, reach)
+        wire[t] = flat32[0:wire_rows, :].astype(BF16)
+        tail32[t, capf:capf + rest, :] = flat32[wire_rows:wire_rows + rest, :]
+
+    pack(offset_at(0, reach, low))
+    pl.semaphore_wait(barrier, n_off - 1)
+    for t in range(n_off):
+        if t != reach:
+            state_copy(t).start()
+    wire_copy(offset_at(0, reach, low)).start()
+
+    @pl.loop(1, n_off - 1)
+    def _(k):
+        t = offset_at(k, reach, low)
         pack(t)
         wire_copy(t).start()
 
@@ -226,12 +229,12 @@
         for r in range(capf):
             i = source_s[t, r]
             il = il_ref[pl.ds(i // n_face, 1), :].astype(BF16)
-            load32[r:r + 1, 0:fu] = -nt(il, outer[i])
-        load_wire[t] = load32[...].astype(BF16)
+            tail32[t, r:r + 1, 0:fu] = -nt(il, outer[i])
+        load_wire[t] = tail32[t].astype(BF16)
 
     @pl.loop(0, n_off - 1)
     def _(k):
-        t = offset_at(k, reach)
+        t = offset_at(k, reach, low)
         pack_loads(t)
         load_copy(t).start()
 
@@ -246,7 +249,7 @@
 
     def add_up(t, received, first):
         who = names(t)
-        spread32[...] = received.astype(F32)
+        spread32[0:wire_rows, :] = received.astype(F32)
         for b in range(0, item_rows, chunk):
             rows = jnp.concatenate(
                 [spread32[pl.ds(b + d, capf, stride=item_rows), :] for d in range(chunk)], axis=1).astype(BF16)
@@ -258,27 +261,45 @@
 
     @pl.loop(0, n_off - 1)
     def _(k):
-        t = near_first(k, reach)
+        t = arrival_at(k, reach, low)
         wire_copy(t).wait_recv()
         add_up(t, arrived[t], False)
 
     @pl.loop(0, n_off - 1)
     def _(k):
-        t = near_first(k, reach)
+        t = arrival_at(k, reach, low)
         load_copy(t).wait_recv()
 
     load_arrived[reach] = load_wire[reach]
     rhs = jnp.zeros(rhs_ref.shape, F32)
-    for t in range(n_off):
-        loads = load_arrived[t].astype(F32)[0:capf, 0:fu].astype(BF16)
-        rhs = rhs + jnp.dot(names(t), loads, preferred_element_type=F32)
+    last = slice((item_rows - rest) * 128, item_rows * 128)
+    ends = schur_ref[:, last]
+    one_row = lax.broadcasted_iota(I32, (owned, 1), 0)
+    for t in range(n_off):
+        tails = load_arrived[t].astype(F32)
+        rhs = rhs + jnp.dot(names(t), tails[0:capf, 0:fu].astype(BF16), preferred_element_type=F32)
+        mine = jnp.where(one_row == owner[t][:, capf - 1:capf], 1.0, 0.0)
+        row = jnp.concatenate([tails[capf + d:capf + d + 1, :] for d in range(rest)], axis=1)
+        ends = ends + mine * row
+    schur_ref[:, last] = ends
     rhs_ref[...] = rhs
 
     @pl.loop(0, n_off - 1)
     def _(k):
-        t = near_first(k, reach)
+        t = arrival_at(k, reach, low)
         wire_copy(t).wait_send()
         load_copy(t).wait_send()
+
+
+def write_out(schur_ref, rhs_ref, schur_hbm, rhs_hbm, sem):
+    copies = [
+        pltpu.make_async_copy(schur_ref, schur_hbm, sem.at[0]),
+        pltpu.make_async_copy(rhs_ref, rhs_hbm, sem.at[1]),
+    ]
+    for c in copies:
+        c.start()
+    for c in copies:
+        c.wait()
 
 
 def per_device(
@@ -295,7 +316,9 @@
     reach = (n_off - 1) // 2
     items = n_elem * n_face
     owned = items // 2
-    wire_rows = -(-(capf * fu * fu // 128) // 16) * 16
+    flat_rows = capf * fu * fu // 128
+    wire_rows = flat_rows // 16 * 16
+    all_rows = -(-flat_rows // 8) * 8
     ins = (
         old_states,
         jnp.swapaxes(send_elem, 1, 2)[0],
@@ -323,13 +346,13 @@
         pltpu.VMEM((n_off, cap, ni), F32),
         pltpu.VMEM((n_elem, ni), F32),
         pltpu.VMEM((capf * fu, 128), F32),
-        pltpu.VMEM((wire_rows, 128), F32),
+        pltpu.VMEM((all_rows, 128), F32),
         pltpu.VMEM((n_off, wire_rows, 128), BF16),
         pltpu.VMEM((n_off, wire_rows, 128), BF16),
-        pltpu.VMEM((16, 128), F32),
+        pltpu.VMEM((n_off, 16, 128), F32),
         pltpu.VMEM((n_off, 16, 128), BF16),
         pltpu.VMEM((n_off, 16, 128), BF16),
-        pltpu.VMEM((wire_rows, 128), F32),
+        pltpu.VMEM((all_rows, 128), F32),
         dma((9,)),
         dma(()),
         dma((n_elem,)),
@@ -350,7 +373,14 @@
             collective_id=0, has_side_effects=True, vmem_limit_bytes=52 * 1024 * 1024),
         name="condense",
     )(*[pltpu.with_memory_space_constraint(a, pltpu.HBM) for a in ins])
-    return sums
+    return pl.pallas_call(
+        write_out,
+        out_shape=tuple(jax.ShapeDtypeStruct(a.shape, a.dtype) for a in sums),
+        in_specs=[pl.BlockSpec(memory_space=pltpu.VMEM)] * 2,
+        out_specs=(pl.BlockSpec(memory_space=pltpu.HBM),) * 2,
+        scratch_shapes=[dma((2,))],
+        name="write_out",
+    )(*[pltpu.with_memory_space_constraint(a, pltpu.VMEM) for a in sums])
 
 
 def solution(mesh):

time: 49.7 us -> 49.2 us (0.990)
  local copies, waits for them, and re-layouts: 1.57 us -> 0 us
  Pallas kernels: 47.4 us -> 48.5 us
    unnamed x2 -> x0, local copies, waits for them, and re-layouts: 1.57 us -> none
    pallas_call x0 -> x1, Pallas kernels: none -> 0.98 us  [per_device(): pl.pallas_call(write_out, out_shape=tuple((jax.ShapeDtypeStruct(a.shape,...]
where the time goes in v3:
time: 49.2 us; the launch traced here: 49.1 us
  Pallas kernels  48.5 us (99%)
  between operations  0.64 us (1%)
    pallas_call x1, Pallas kernels, per_device(): pl.pallas_call(functools.partial(kernel, dims), out_shape=(jax.ShapeDtype...  47.5 us

profile of v3, /device:TPU:1, one launch (start us, length us, event | category | flops | bytes accessed | tf_op | source)
XLA Modules:
  0.0 49.1 jit_solution(9179723371481059491)
XLA Ops:
  0.6 47.5 %condense.1 = (f32[40,6400]{1,0:T(8,128)S(1)}, f32[40,80]{1,0:T(8,128)S(1)}) custom-call(bf16[16,320]{1,0:T(8,128)(2,1)} %states_hbm.1, s32[8,9]{1,0:T(8,128)} %bitcast.16, s32[4,16]{1,0:T(4,128)} %bitcast.19, s32[1,16]{1,0:T(1,128)} %bitcast.21, f32[4,16]{1,0:T(4,128)} %bitcast.20, bf16[16,320,320]{2,1,0:T(8,128)(2,1)} %inverse_hbm.1, ...), custom_call_target="tpu_custom_call" | custom-call | tf_op jit(solution)/shard_map/condense/pallas_call | solution.py:363
  48.1 1.0 %write_out.1 = (f32[40,6400]{1,0:T(8,128)}, f32[40,80]{1,0:T(8,128)}) custom-call(f32[40,6400]{1,0:T(8,128)S(1)} %get-tuple-element.4.schur_ref, f32[40,80]{1,0:T(8,128)S(1)} %get-tuple-element.5.rhs_ref), custom_call_target="tpu_custom_call" | custom-call | tf_op jit(solution)/shard_map/write_out/pallas_call | solution.py:376

commit v4 on v3

--- a/solution.py
+++ b/solution.py
@@ -17,17 +17,28 @@
     return lax.dot_general(a, b, NT, preferred_element_type=F32)
 
 
-def offset_at(k, reach, low):
-    back = k // reach
-    size = reach - (k - back * reach)
-    return reach + (1 - 2 * low) * (1 - 2 * back) * size
-
-
-def arrival_at(k, reach, low):
-    back = k // reach
-    size = k - back * reach + 1
-    sign = (1 - 2 * low) * (1 - 2 * back)
-    return reach + sign * size
+def at_least(a, b):
+    return (a - b + 64) // 64
+
+
+def offset_at(k, reach, u):
+    out_up = at_least(u, k)
+    first = out_up * (reach - u + k) - (1 - out_up) * k
+    rest = k - reach - 1
+    in_up = 1 - at_least(rest, reach - 1 - u)
+    second = in_up * (rest + 1) - (1 - in_up) * (rest + u - reach + 2)
+    is_second = at_least(k, reach + 1)
+    return reach + (1 - is_second) * first + is_second * second
+
+
+def arrival_at(k, reach, u):
+    near_up = 1 - at_least(k, u)
+    first = near_up * (k + 1) - (1 - near_up) * (k - u + 1)
+    rest = k - reach + 1
+    down = at_least(u, rest)
+    second = (1 - down) * rest - down * (reach - u + rest)
+    is_second = at_least(k, reach - 1)
+    return reach + (1 - is_second) * first + is_second * second
 
 
 def kernel(
@@ -36,7 +47,7 @@
     mass_hbm, scale_hbm, shift_hbm, owner_hbm,
     schur_ref, rhs_ref,
     states, send_e, slot, count, weight, inverse, inner, outer, mass, scale, shift, owner,
-    mapped, source_v, source_s, st_send, st_recv, il_ref, block32, flat32, wire, arrived,
+    mapped, source_v, source_s, st_send, st_recv, il_ref, all_ref, by_face, block32, flat32, wire, arrived,
     tail32, load_wire, load_arrived, spread32,
     small_sem, source_sem, inverse_sem, inner_sem, outer_sem,
     st_ssem, st_rsem, w_ssem, w_rsem, l_ssem, l_rsem,
@@ -48,7 +59,7 @@
     wire_rows = wire.shape[1]
     rest = capf * item_rows - wire_rows
     me = lax.axis_index("dom")
-    low = 1 - lax.rem(me, 2 * reach) // reach
+    u = lax.rem(me, reach)
 
     smalls = [
         pltpu.make_async_copy(a, b, small_sem.at[q])
@@ -185,16 +196,16 @@
         wire[t] = flat32[0:wire_rows, :].astype(BF16)
         tail32[t, capf:capf + rest, :] = flat32[wire_rows:wire_rows + rest, :]
 
-    pack(offset_at(0, reach, low))
     pl.semaphore_wait(barrier, n_off - 1)
     for t in range(n_off):
         if t != reach:
             state_copy(t).start()
-    wire_copy(offset_at(0, reach, low)).start()
+    pack(offset_at(0, reach, u))
+    wire_copy(offset_at(0, reach, u)).start()
 
     @pl.loop(1, n_off - 1)
     def _(k):
-        t = offset_at(k, reach, low)
+        t = offset_at(k, reach, u)
         pack(t)
         wire_copy(t).start()
 
@@ -221,20 +232,42 @@
     row_of = lax.broadcasted_iota(I32, (n_elem, ni), 0)
     il_ref[...] = jnp.zeros_like(il_ref)
 
-    @pl.loop(0, n_elem)
-    def _(n):
-        il_ref[...] += jnp.where(row_of == n, nt(projected, inverse[n]), 0.0)
+    together = 4
+
+    @pl.loop(0, n_elem // together)
+    def _(g):
+        part = jnp.zeros((n_elem, ni), F32)
+        for d in range(together):
+            n = g * together + d
+            part = part + jnp.where(row_of == n, nt(projected, inverse[n]), 0.0)
+        il_ref[...] += part
+
+    il = il_ref[...].astype(BF16)
+    row_nf = lax.broadcasted_iota(I32, (n_elem, n_face * fu), 0)
+    all_ref[...] = jnp.zeros_like(all_ref)
+
+    @pl.loop(0, n_elem // together)
+    def _(g):
+        part = jnp.zeros((n_elem, n_face * fu), F32)
+        for d in range(together):
+            n = g * together + d
+            rows = outer[pl.ds(n * n_face, n_face)].reshape(n_face * fu, ni)
+            part = part - jnp.where(row_nf == n, nt(il, rows), 0.0)
+        all_ref[...] += part
+
+    for j in range(n_face):
+        by_face[j * n_elem:(j + 1) * n_elem, 0:fu] = all_ref[:, j * fu:(j + 1) * fu]
 
     def pack_loads(t):
         for r in range(capf):
             i = source_s[t, r]
-            il = il_ref[pl.ds(i // n_face, 1), :].astype(BF16)
-            tail32[t, r:r + 1, 0:fu] = -nt(il, outer[i])
+            row = i % n_face * n_elem + i // n_face
+            tail32[t, r:r + 1, 0:fu] = by_face[pl.ds(row, 1), 0:fu]
         load_wire[t] = tail32[t].astype(BF16)
 
     @pl.loop(0, n_off - 1)
     def _(k):
-        t = offset_at(k, reach, low)
+        t = offset_at(k, reach, u)
         pack_loads(t)
         load_copy(t).start()
 
@@ -261,13 +294,13 @@
 
     @pl.loop(0, n_off - 1)
     def _(k):
-        t = arrival_at(k, reach, low)
+        t = arrival_at(k, reach, u)
         wire_copy(t).wait_recv()
         add_up(t, arrived[t], False)
 
     @pl.loop(0, n_off - 1)
     def _(k):
-        t = arrival_at(k, reach, low)
+        t = arrival_at(k, reach, u)
         load_copy(t).wait_recv()
 
     load_arrived[reach] = load_wire[reach]
@@ -286,7 +319,7 @@
 
     @pl.loop(0, n_off - 1)
     def _(k):
-        t = arrival_at(k, reach, low)
+        t = arrival_at(k, reach, u)
         wire_copy(t).wait_send()
         load_copy(t).wait_send()
 
@@ -345,6 +378,8 @@
         pltpu.VMEM((n_off, cap, ni), F32),
         pltpu.VMEM((n_off, cap, ni), F32),
         pltpu.VMEM((n_elem, ni), F32),
+        pltpu.VMEM((n_elem, n_face * fu), F32),
+        pltpu.VMEM((items, 128), F32),
         pltpu.VMEM((capf * fu, 128), F32),
         pltpu.VMEM((all_rows, 128), F32),
         pltpu.VMEM((n_off, wire_rows, 128), BF16),

time: 49.2 us -> 48 us (0.976)
  Pallas kernels: 48.5 us -> 47.3 us
    pallas_call x1, Pallas kernels: 47.5 us -> 46.3 us  [per_device(): pl.pallas_call(functools.partial(kernel, dims), out_shape=(jax.ShapeDtype...]
where the time goes in v4:
time: 48 us
  Pallas kernels  47.3 us (99%)
  between operations  0.64 us (1%)
    pallas_call x1, Pallas kernels, per_device(): pl.pallas_call(functools.partial(kernel, dims), out_shape=(jax.ShapeDtype...  46.3 us
    pallas_call x1, Pallas kernels, per_device(): pl.pallas_call(write_out, out_shape=tuple((jax.ShapeDtypeStruct(a.shape,...  0.98 us

profile of v4, /device:TPU:1, one launch (start us, length us, event | category | flops | bytes accessed | tf_op | source)
XLA Modules:
  0.0 48.0 jit_solution(17323146627108479587)
XLA Ops:
  0.6 46.3 %condense.1 = (f32[40,6400]{1,0:T(8,128)S(1)}, f32[40,80]{1,0:T(8,128)S(1)}) custom-call(bf16[16,320]{1,0:T(8,128)(2,1)} %states_hbm.1, s32[8,9]{1,0:T(8,128)} %bitcast.16, s32[4,16]{1,0:T(4,128)} %bitcast.19, s32[1,16]{1,0:T(1,128)} %bitcast.21, f32[4,16]{1,0:T(4,128)} %bitcast.20, bf16[16,320,320]{2,1,0:T(8,128)(2,1)} %inverse_hbm.1, ...), custom_call_target="tpu_custom_call" | custom-call | tf_op jit(solution)/shard_map/condense/pallas_call | solution.py:398
  47.0 1.0 %write_out.1 = (f32[40,6400]{1,0:T(8,128)}, f32[40,80]{1,0:T(8,128)}) custom-call(f32[40,6400]{1,0:T(8,128)S(1)} %get-tuple-element.4.schur_ref, f32[40,80]{1,0:T(8,128)S(1)} %get-tuple-element.5.rhs_ref), custom_call_target="tpu_custom_call" | custom-call | tf_op jit(solution)/shard_map/write_out/pallas_call | solution.py:411

commit v5 on v4

--- a/solution.py
+++ b/solution.py
@@ -144,7 +144,7 @@
     e_row = lax.broadcasted_iota(I32, (n_elem, cap), 0)
     for t in range(n_off):
         sel = jnp.where(e_row == jnp.broadcast_to(picks[:, t:t + 1].reshape(1, cap), (n_elem, cap)), 1.0, 0.0)
-        st_send[t] = lax.dot_general(sel.astype(BF16), old, TN, preferred_element_type=F32)
+        st_send[t] = lax.dot_general(sel.astype(BF16), old, TN, preferred_element_type=F32).astype(BF16)
 
     def state_copy(t):
         return pltpu.make_async_remote_copy(
@@ -226,7 +226,7 @@
         at = jnp.broadcast_to(slot[k:k + 1, :], (n_slot, n_elem)) == q_row
         mix = mix + jnp.where(at, jnp.broadcast_to(w, (n_slot, n_elem)), 0.0)
     mix_t = jnp.transpose(mix)
-    gathered = st_recv[...].reshape(n_slot, ni)
+    gathered = st_recv[...].astype(F32).reshape(n_slot, ni)
     top = jnp.dot(mix_t, gathered, precision=lax.Precision.HIGHEST, preferred_element_type=F32)
     projected = (top / jnp.sum(mix_t, axis=1, keepdims=True)).astype(BF16)
     row_of = lax.broadcasted_iota(I32, (n_elem, ni), 0)
@@ -375,8 +375,8 @@
         pltpu.VMEM((items, fu, ni), BF16),
         pltpu.VMEM((16, 128), I32),
         pltpu.SMEM((16, 128), I32),
-        pltpu.VMEM((n_off, cap, ni), F32),
-        pltpu.VMEM((n_off, cap, ni), F32),
+        pltpu.VMEM((n_off, cap, ni), BF16),
+        pltpu.VMEM((n_off, cap, ni), BF16),
         pltpu.VMEM((n_elem, ni), F32),
         pltpu.VMEM((n_elem, n_face * fu), F32),
         pltpu.VMEM((items, 128), F32),

time: 48 us -> 47.3 us (0.985)
  Pallas kernels: 47.3 us -> 46.6 us
    pallas_call x1, Pallas kernels: 46.3 us -> 45.6 us  [per_device(): pl.pallas_call(functools.partial(kernel, dims), out_shape=(jax.ShapeDtype...]
where the time goes in v5:
time: 47.3 us
  Pallas kernels  46.6 us (99%)
  between operations  0.64 us (1%)
    pallas_call x1, Pallas kernels, per_device(): pl.pallas_call(functools.partial(kernel, dims), out_shape=(jax.ShapeDtype...  45.6 us
    pallas_call x1, Pallas kernels, per_device(): pl.pallas_call(write_out, out_shape=tuple((jax.ShapeDtypeStruct(a.shape,...  0.98 us

profile of v5, /device:TPU:1, one launch (start us, length us, event | category | flops | bytes accessed | tf_op | source)
XLA Modules:
  0.0 47.3 jit_solution(15962444048458051199)
XLA Ops:
  0.6 45.6 %condense.1 = (f32[40,6400]{1,0:T(8,128)S(1)}, f32[40,80]{1,0:T(8,128)S(1)}) custom-call(bf16[16,320]{1,0:T(8,128)(2,1)} %states_hbm.1, s32[8,9]{1,0:T(8,128)} %bitcast.16, s32[4,16]{1,0:T(4,128)} %bitcast.19, s32[1,16]{1,0:T(1,128)} %bitcast.21, f32[4,16]{1,0:T(4,128)} %bitcast.20, bf16[16,320,320]{2,1,0:T(8,128)(2,1)} %inverse_hbm.1, ...), custom_call_target="tpu_custom_call" | custom-call | tf_op jit(solution)/shard_map/condense/pallas_call | solution.py:398
  46.3 1.0 %write_out.1 = (f32[40,6400]{1,0:T(8,128)}, f32[40,80]{1,0:T(8,128)}) custom-call(f32[40,6400]{1,0:T(8,128)S(1)} %get-tuple-element.4.schur_ref, f32[40,80]{1,0:T(8,128)S(1)} %get-tuple-element.5.rhs_ref), custom_call_target="tpu_custom_call" | custom-call | tf_op jit(solution)/shard_map/write_out/pallas_call | solution.py:411

commit v6 on v5

--- a/solution.py
+++ b/solution.py
@@ -232,7 +232,7 @@
     row_of = lax.broadcasted_iota(I32, (n_elem, ni), 0)
     il_ref[...] = jnp.zeros_like(il_ref)
 
-    together = 4
+    together = 8
 
     @pl.loop(0, n_elem // together)
     def _(g):

time: 47.3 us -> 47.4 us (level)
  no operation moved by 1% of the time
where the time goes in v6:
time: 47.4 us; the launch traced here: 47.3 us
  Pallas kernels  46.6 us (98%)
  between operations  0.64 us (1%)
    pallas_call x1, Pallas kernels, per_device(): pl.pallas_call(functools.partial(kernel, dims), out_shape=(jax.ShapeDtype...  45.6 us
    pallas_call x1, Pallas kernels, per_device(): pl.pallas_call(write_out, out_shape=tuple((jax.ShapeDtypeStruct(a.shape,...  0.98 us

profile of v6, /device:TPU:1, one launch (start us, length us, event | category | flops | bytes accessed | tf_op | source)
XLA Modules:
  0.0 47.3 jit_solution(9055856355669017830)
XLA Ops:
  0.6 45.6 %condense.1 = (f32[40,6400]{1,0:T(8,128)S(1)}, f32[40,80]{1,0:T(8,128)S(1)}) custom-call(bf16[16,320]{1,0:T(8,128)(2,1)} %states_hbm.1, s32[8,9]{1,0:T(8,128)} %bitcast.16, s32[4,16]{1,0:T(4,128)} %bitcast.19, s32[1,16]{1,0:T(1,128)} %bitcast.21, f32[4,16]{1,0:T(4,128)} %bitcast.20, bf16[16,320,320]{2,1,0:T(8,128)(2,1)} %inverse_hbm.1, ...), custom_call_target="tpu_custom_call" | custom-call | tf_op jit(solution)/shard_map/condense/pallas_call | solution.py:398
  46.3 1.0 %write_out.1 = (f32[40,6400]{1,0:T(8,128)}, f32[40,80]{1,0:T(8,128)}) custom-call(f32[40,6400]{1,0:T(8,128)S(1)} %get-tuple-element.4.schur_ref, f32[40,80]{1,0:T(8,128)S(1)} %get-tuple-element.5.rhs_ref), custom_call_target="tpu_custom_call" | custom-call | tf_op jit(solution)/shard_map/write_out/pallas_call | solution.py:411
